TPU v7x, 32 devices: a whole 2x2x4 slice. The times are simulated.
32 devices in a mesh: gx: 16 (over z, y, x), gy: 2 (over core).
Axes of the slice: x: 2, y: 2, z: 4, core: 2. Of those that a mesh axis runs over, the one named last changes fastest.
Arguments:
- history: bfloat16 [128, 2048, 256], P(('gx', 'gy')), may hold values from -100 to 100
- lengths: int32 [128], P(('gx', 'gy')), may hold values from 16 to 2048
- candidates: int32 [128, 64], P(('gx', 'gy')), may hold values from 0 to 131071, as said below
- item_table: bfloat16 [131072, 512], P(('gx', 'gy')), may hold values from -6 to 6
- value_weight: bfloat16 [256, 256], replicated, may hold values from -0.375 to 0.375
- click_hidden: bfloat16 [768, 256], replicated, may hold values from -0.21875 to 0.21875
- convert_hidden: bfloat16 [768, 256], replicated, may hold values from -0.21875 to 0.21875
- click_output: bfloat16 [256], replicated, may hold values from -0.75 to 0.75
- convert_output: bfloat16 [256], replicated, may hold values from -0.75 to 0.75
Outputs:
- click_rate: float32 [128, 64], P(('gx', 'gy'))
- click_conversion: float32 [128, 64], P(('gx', 'gy'))
Inputs may be any that keep to these rules, and one draw needn't show every extreme that they name: Device k holds the table rows k * 4096 to (k + 1) * 4096 - 1. Of the 256 candidates of one device, at most 16 are items of one device's rows, and exactly 16 are items of some device's rows.
All inputs are finite; a program needn't handle non-finite values.
Results may differ from a plain program's by a relative error of at most 0.0028.
Values may be sent and summed in bfloat16 or wider, within the bound.
A program may use at most 64 MiB of HBM per device.

v0:
```python
import functools
import math

import jax
import jax.numpy as jnp
from jax import lax
from jax.experimental import pallas as pl
from jax.experimental.pallas import tpu as pltpu
from jax.sharding import PartitionSpec as P

HEADS = 4
CHUNK = 512
SPLIT = 256
MESH = pl.DeviceIdType.MESH
neg_big = -1e30
f32, bf16 = jnp.float32, jnp.bfloat16


def dot(a, b, dims=((1,), (0,))):
    return lax.dot_general(a, b, (dims, ((), ())), preferred_element_type=f32)


def iota(shape, axis):
    return lax.broadcasted_iota(jnp.int32, shape, axis)


def fused_kernel(
    n,
    ny,
    cap,
    len_ref,
    cand_ref,
    click_out_ref,
    convert_out_ref,
    table_hbm,
    hist_hbm,
    value_hbm,
    click_hbm,
    convert_hbm,
    rate_ref,
    both_ref,
    table,
    hist,
    value,
    click,
    convert,
    id_send,
    id_recv,
    pick,
    target_send,
    target_recv,
    feature_send,
    feature_recv,
    scores,
    tops,
    joined,
    load_sems,
    sems,
):
    me = lax.axis_index("gx") * ny + lax.axis_index("gy")
    users, per_user = cand_ref.shape
    seq, width = hist.shape[1:]
    total = users * per_user
    table_rows = table.shape[0]

    loads = [
        pltpu.make_async_copy(src, dst, load_sems.at[i])
        for i, (src, dst) in enumerate(
            [(table_hbm, table), (value_hbm, value), (click_hbm, click), (convert_hbm, convert)]
            + [(hist_hbm.at[u], hist.at[u]) for u in range(users)]
        )
    ]
    loads[0].start()

    def at(j):
        d = lax.rem(me + j, n)
        return d, (lax.div(d, ny), lax.rem(d, ny))

    barrier = pltpu.get_barrier_semaphore()

    def greet(j, c):
        pl.semaphore_signal(barrier, inc=1, device_id=at(j)[1], device_id_type=MESH)
        return c

    lax.fori_loop(1, n, greet, 0)
    for load in loads[4:] + loads[1:4]:
        load.start()

    ids = jnp.concatenate([cand_ref[u : u + 1, :] for u in range(users)], axis=1)
    first = iota((n, total), 0) * table_rows
    local = ids - first
    mine = (local >= 0) & (local < table_rows)
    hot = jnp.where(mine, 1.0, 0.0).astype(f32)
    earlier = jnp.where(iota((total, total), 0) < iota((total, total), 1), 1.0, 0.0).astype(bf16)
    rank = jnp.sum(hot * dot(hot.astype(bf16), earlier), axis=0, keepdims=True)
    owner = jnp.sum(hot * iota((n, total), 0).astype(f32), axis=0, keepdims=True)
    slot = owner * cap + rank
    high = jnp.where(mine, local // SPLIT, 0).astype(f32).astype(bf16)
    low = jnp.where(mine, local % SPLIT, 0).astype(f32).astype(bf16)
    rank_i = rank.astype(jnp.int32)
    lane = iota((128, total), 0)
    at_high = jnp.where(lane == rank_i, 1.0, 0.0).astype(bf16)
    at_low = jnp.where(lane == rank_i + cap, 1.0, 0.0).astype(bf16)
    request = dot(high, at_high, ((1,), (1,))) + dot(low, at_low, ((1,), (1,)))
    for d in range(n):
        id_send[d] = request[d : d + 1, :]

    def send(src, dst, lo, hi, sem, by_owner):
        def one(j, c):
            d, where = at(j)
            pltpu.make_async_remote_copy(
                src_ref=src.at[d if by_owner else j],
                dst_ref=dst.at[me],
                send_sem=sems.at[sem],
                recv_sem=sems.at[sem + 1],
                device_id=where,
                device_id_type=MESH,
            ).start()
            return c

        lax.fori_loop(max(lo, 1), hi, one, 0)

    others = pl.ds(0, n - 1)

    def drain(ref, sem):
        pltpu.make_async_copy(ref.at[others], ref.at[others], sems.at[sem]).wait()

    pl.semaphore_wait(barrier, n - 1)
    send(id_send, id_recv, 1, n, 0, True)
    id_recv[me] = id_send[me]

    same = iota((total, total), 0) == iota((total, total), 1)
    slot_col = jnp.sum(jnp.where(same, slot, 0.0), axis=1, keepdims=True).astype(jnp.int32)
    choose = jnp.where(slot_col == iota((total, n * cap), 1), 1.0, 0.0).astype(bf16)

    drain(id_recv, 1)
    group = 256 // cap
    asked = jnp.concatenate([id_recv[d] for d in range(n)], axis=0).astype(bf16)
    loads[0].wait()
    for g in range(n // group):
        base = g * group
        source = lax.rem(me + base + iota((256, n), 0) // cap, n)
        expand = jnp.where(source == iota((256, n), 1), 1.0, 0.0).astype(bf16)
        spread = dot(expand, asked)
        place = iota((256, 128), 0) % cap
        lane = iota((256, 128), 1)
        weight = jnp.where(lane == place, float(SPLIT), jnp.where(lane == place + cap, 1.0, 0.0))
        wanted = jnp.sum(spread * weight, axis=1, keepdims=True).astype(jnp.int32)
        pick[g] = jnp.where(wanted == iota((256, table_rows), 1), 1.0, 0.0).astype(bf16)
        found = dot(pick[g], table[:, :width]).astype(bf16)
        for k in range(group):
            target_send[base + k] = found[k * cap : (k + 1) * cap, :]
        send(target_send, target_recv, base, base + group, 2, False)
    for g in range(n // group):
        base = g * group
        found = dot(pick[g], table[:, width:]).astype(bf16)
        for k in range(group):
            feature_send[base + k] = found[k * cap : (k + 1) * cap, :]
        send(feature_send, feature_recv, base, base + group, 4, False)
    target_recv[me] = target_send[0]
    feature_recv[me] = feature_send[0]

    for load in loads[1:]:
        load.wait()
    drain(target_recv, 3)
    target = dot(choose, target_recv[...].reshape(n * cap, width)).astype(bf16)
    joined[:, width : 2 * width] = target

    head = width // HEADS
    queries = HEADS * per_user
    scale = math.log2(math.e) / math.sqrt(head)
    lane_head = iota((per_user, width), 1) // head
    chunks = seq // CHUNK
    slabs = CHUNK // 128

    def query_of(u):
        own = target[u * per_user : (u + 1) * per_user, :]
        return jnp.concatenate(
            [jnp.where(lane_head == h, own, jnp.zeros_like(own)) for h in range(HEADS)], axis=0
        )

    def score(u, c, query, top):
        s = dot(query, hist[u, c * CHUNK : (c + 1) * CHUNK, :], ((1,), (1,))) * scale
        live = iota((queries, CHUNK), 1) < len_ref[u] - c * CHUNK
        s = jnp.where(live, s, neg_big)
        scores[u % 2, :, c * CHUNK : (c + 1) * CHUNK] = s
        for k in range(slabs):
            part = s[:, k * 128 : (k + 1) * 128]
            top = part if top is None else jnp.maximum(top, part)
        return top

    def finish(u, top):
        tops[u % 2] = jnp.broadcast_to(jnp.max(top, axis=1, keepdims=True), (queries, 128))

    def gather(u, c, total_weight, context):
        top = tops[u % 2]
        parts = []
        for k in range(slabs):
            at_k = c * CHUNK + k * 128
            w = jnp.exp2(scores[u % 2, :, at_k : at_k + 128] - top).astype(bf16)
            wide = w.astype(f32)
            total_weight = wide if total_weight is None else total_weight + wide
            parts.append(w)
        more = dot(jnp.concatenate(parts, axis=1), hist[u, c * CHUNK : (c + 1) * CHUNK, :])
        return total_weight, more if context is None else context + more

    def interest(u, total_weight, context):
        part0 = context.astype(bf16)
        rest = context - part0.astype(f32)
        part1 = rest.astype(bf16)
        part2 = (rest - part1.astype(f32)).astype(bf16)
        full = dot(part0, value[...]) + dot(part1, value[...]) + dot(part2, value[...])
        full = full / jnp.sum(total_weight, axis=1, keepdims=True)
        pooled = jnp.zeros((per_user, width), f32)
        for h in range(HEADS):
            pooled = jnp.where(lane_head == h, full[h * per_user : (h + 1) * per_user, :], pooled)
        normed = pooled * lax.rsqrt(jnp.mean(pooled * pooled, axis=1, keepdims=True) + 1e-6)
        joined[u * per_user : (u + 1) * per_user, :width] = normed.astype(bf16)

    query = query_of(0)
    top = None
    for c in range(chunks):
        top = score(0, c, query, top)
    finish(0, top)
    for u in range(users):
        if u + 1 < users:
            query = query_of(u + 1)
        top = total_weight = context = None
        for c in range(chunks):
            if u + 1 < users:
                top = score(u + 1, c, query, top)
            total_weight, context = gather(u, c, total_weight, context)
        if u + 1 < users:
            finish(u + 1, top)
        interest(u, total_weight, context)

    drain(feature_recv, 5)
    feature = dot(choose, feature_recv[...].reshape(n * cap, width))
    joined[:, 2 * width :] = feature.astype(bf16)
    every = joined[...]

    def tower(hidden, output_ref):
        act = jnp.maximum(dot(every, hidden[...]), 0.0).astype(bf16)
        last = output_ref[...].reshape(1, -1)
        return 1.0 / (1.0 + jnp.exp(-dot(last, act, ((1,), (1,)))))

    rate = tower(click, click_out_ref)
    both = rate * tower(convert, convert_out_ref)
    for u in range(users):
        own = slice(u * per_user, (u + 1) * per_user)
        rate_ref[u : u + 1, :] = rate[:, own]
        both_ref[u : u + 1, :] = both[:, own]
    drain(id_send, 0)
    drain(target_send, 2)
    drain(feature_send, 4)


def local(
    n,
    ny,
    history,
    lengths,
    candidates,
    item_table,
    value_weight,
    click_hidden,
    convert_hidden,
    click_output,
    convert_output,
):
    users, per_user = candidates.shape
    seq, width = history.shape[1:]
    total = users * per_user
    cap = max(2 * total // n, 16)
    queries = HEADS * per_user
    vmem = pl.BlockSpec(memory_space=pltpu.VMEM)
    hbm = pl.BlockSpec(memory_space=pl.ANY)
    out = jax.ShapeDtypeStruct((users, per_user), f32)
    slab = pltpu.VMEM((n, cap, width), bf16)
    held = [item_table, history, value_weight, click_hidden, convert_hidden]
    return pl.pallas_call(
        functools.partial(fused_kernel, n, ny, cap),
        out_shape=(out, out),
        in_specs=[pl.BlockSpec(memory_space=pltpu.SMEM)] + [vmem] * 3 + [hbm] * 5,
        out_specs=(vmem, vmem),
        scratch_shapes=[pltpu.VMEM(x.shape, x.dtype) for x in held]
        + [
            pltpu.VMEM((n, 1, 128), f32),
            pltpu.VMEM((n, 1, 128), f32),
            pltpu.VMEM((n * cap // 256, 256, item_table.shape[0]), bf16),
            slab,
            slab,
            slab,
            slab,
            pltpu.VMEM((2, queries, seq), f32),
            pltpu.VMEM((2, queries, 128), f32),
            pltpu.VMEM((total, 3 * width), bf16),
            pltpu.SemaphoreType.DMA((4 + users,)),
            pltpu.SemaphoreType.DMA((6,)),
        ],
        compiler_params=pltpu.CompilerParams(collective_id=0, has_side_effects=True),
        name="esmm",
    )(lengths, candidates, click_output, convert_output, *held)


def solution(mesh):
    both = ("gx", "gy")
    placed = (P(both, None, None), P(both), P(both, None), P(both, None), P(), P(), P(), P(), P())
    return jax.shard_map(
        functools.partial(local, mesh.shape["gx"] * mesh.shape["gy"], mesh.shape["gy"]),
        mesh=mesh,
        in_specs=placed,
        out_specs=(P(both, None), P(both, None)),
        check_vma=False,
    )
```

profile of v0, /device:TPU:13, one launch (start us, length us, event | category | flops | bytes accessed | tf_op | source)
XLA Modules:
  0.0 32.3 jit_solution(1595389926566344167)
XLA Ops:
  0.6 29.1 %esmm.1 = (f32[4,64]{1,0:T(4,128)}, f32[4,64]{1,0:T(4,128)}) custom-call(s32[4]{0:T(128)} %len_ref.1, s32[4,64]{1,0:T(4,128)} %cand_ref.1, bf16[256]{0:T(256)(128)(2,1)} %click_out_ref.1, bf16[256]{0:T(256)(128)(2,1)} %convert_out_ref.1, bf16[4096,512]{1,0:T(8,128)(2,1)} %table_hbm.1, bf16[4,2048,256]{2,1,0:T(8,128)(2,1)} %hist_hbm.1, ...), custom_call_target="tpu_custom_call" | custom-call | tf_op jit(solution)/shard_map/esmm/pallas_call | solution.py:281
  29.8 1.2 %copy.13 = f32[4,64]{1,0:T(4,128)} copy(f32[4,64]{1,0:T(4,128)} %get-tuple-element.4) | data formatting | bytes 2048
  31.0 1.2 %copy.14 = f32[4,64]{1,0:T(4,128)} copy(f32[4,64]{1,0:T(4,128)} %get-tuple-element.5) | data formatting | bytes 2048
where the time goes:
time: 32.5 us; the launch traced here: 32.3 us
  Pallas kernels  29.1 us (90%)
  local copies, waits for them, and re-layouts  2.48 us (8%)
  between operations  0.64 us (2%)
    pallas_call x1, Pallas kernels, local(): pl.pallas_call(functools.partial(fused_kernel, n, ny, cap), out_shape=(ou...  29.1 us
    unnamed x2, local copies, waits for them, and re-layouts  2.48 us

commit v1 on v0

v1 whole, which is shorter than its diff:
```python
import functools
import math

import jax
import jax.numpy as jnp
from jax import lax
from jax.experimental import pallas as pl
from jax.experimental.pallas import tpu as pltpu
from jax.sharding import PartitionSpec as P

HEADS = 4
CHUNK = 512
SPLIT = 256
MESH = pl.DeviceIdType.MESH
neg_big = -1e30
f32, bf16 = jnp.float32, jnp.bfloat16


def dot(a, b, dims=((1,), (0,))):
    return lax.dot_general(a, b, (dims, ((), ())), preferred_element_type=f32)


def iota(shape, axis):
    return lax.broadcasted_iota(jnp.int32, shape, axis)


def fused_kernel(
    n,
    ny,
    cap,
    cand_hbm,
    len_hbm,
    click_out_hbm,
    convert_out_hbm,
    table_hbm,
    hist_hbm,
    value_hbm,
    click_hbm,
    convert_hbm,
    logit_ref,
    cand_ref,
    len_ref,
    click_out_ref,
    convert_out_ref,
    table,
    hist,
    value,
    click,
    convert,
    id_send,
    id_recv,
    pick,
    target_send,
    target_recv,
    feature_send,
    feature_recv,
    scores,
    weights,
    keyed,
    hidden_t,
    partial,
    interest_t,
    load_sems,
    sems,
):
    me = lax.axis_index("gx") * ny + lax.axis_index("gy")
    users, per_user = cand_ref.shape
    seq, width = hist.shape[1:]
    total = users * per_user
    table_rows = table.shape[0]
    plane = n // 4
    me_z = lax.div(me, plane)
    me_r = lax.rem(me, plane)
    half = lax.div(me_z, 2)
    planes = (3 - 3 * half, 2 - half, 2 * half + 1 - lax.rem(me_z, 2), me_z)

    def at(q, k):
        d = planes[q] * plane + lax.rem(me_r + k, plane)
        return d, (lax.div(d, ny), lax.rem(d, ny))

    def each(lo, hi, body):
        for q in range(4):
            first, last = max(lo - q * plane, q // 3), min(hi - q * plane, plane)
            if first < last:
                lax.fori_loop(first, last, functools.partial(body, q), 0)

    barrier = pltpu.get_barrier_semaphore()

    def greet(q, k, c):
        pl.semaphore_signal(barrier, inc=1, device_id=at(q, k)[1], device_id_type=MESH)
        return c

    loads = [
        pltpu.make_async_copy(src, dst, load_sems.at[i])
        for i, (src, dst) in enumerate(
            [
                (cand_hbm, cand_ref),
                (table_hbm, table),
                (len_hbm, len_ref),
                (click_out_hbm, click_out_ref),
                (convert_out_hbm, convert_out_ref),
                (value_hbm, value),
                (click_hbm, click),
                (convert_hbm, convert),
            ]
            + [(hist_hbm.at[u], hist.at[u]) for u in range(users)]
        )
    ]
    loads[0].start()
    each(0, n, greet)
    for load in loads[1:]:
        load.start()
    loads[0].wait()

    ids = jnp.concatenate([cand_ref[u : u + 1, :] for u in range(users)], axis=1)
    first = iota((n, total), 0) * table_rows
    local = ids - first
    mine = (local >= 0) & (local < table_rows)
    hot = jnp.where(mine, 1.0, 0.0).astype(f32)
    earlier = jnp.where(iota((total, total), 0) < iota((total, total), 1), 1.0, 0.0).astype(bf16)
    rank = jnp.sum(hot * dot(hot.astype(bf16), earlier), axis=0, keepdims=True)
    owner = jnp.sum(hot * iota((n, total), 0).astype(f32), axis=0, keepdims=True)
    slot = owner * cap + rank
    high = jnp.where(mine, local // SPLIT, 0).astype(f32).astype(bf16)
    low = jnp.where(mine, local % SPLIT, 0).astype(f32).astype(bf16)
    rank_i = rank.astype(jnp.int32)
    lane = iota((128, total), 0)
    at_high = jnp.where(lane == rank_i, 1.0, 0.0).astype(bf16)
    at_low = jnp.where(lane == rank_i + cap, 1.0, 0.0).astype(bf16)
    request = dot(high, at_high, ((1,), (1,))) + dot(low, at_low, ((1,), (1,)))
    for d in range(n):
        id_send[d] = request[d : d + 1, :]

    def send(src, dst, lo, hi, sem, by_owner):
        def one(q, k, c):
            d, where = at(q, k)
            pltpu.make_async_remote_copy(
                src_ref=src.at[d if by_owner else q * plane + k],
                dst_ref=dst.at[me],
                send_sem=sems.at[sem],
                recv_sem=sems.at[sem + 1],
                device_id=where,
                device_id_type=MESH,
            ).start()
            return c

        each(lo, hi, one)

    others = pl.ds(0, n - 1)

    def drain(ref, sem):
        pltpu.make_async_copy(ref.at[others], ref.at[others], sems.at[sem]).wait()

    pl.semaphore_wait(barrier, n - 1)
    send(id_send, id_recv, 0, n, 0, True)
    id_recv[me] = id_send[me]

    same = iota((total, total), 0) == iota((total, total), 1)
    slot_col = jnp.sum(jnp.where(same, slot, 0.0), axis=1, keepdims=True).astype(jnp.int32)
    choose = jnp.where(slot_col == iota((total, n * cap), 1), 1.0, 0.0).astype(bf16)

    drain(id_recv, 1)
    group = 256 // cap
    asked = jnp.concatenate([id_recv[d] for d in range(n)], axis=0).astype(bf16)
    loads[1].wait()
    for g in range(n // group):
        base = g * group
        turn = base + iota((256, n), 0) // cap
        quarter = turn // plane
        source = jnp.where(quarter == 0, planes[0], planes[3])
        source = jnp.where(quarter == 1, planes[1], jnp.where(quarter == 2, planes[2], source))
        source = source * plane + lax.rem(me_r + turn % plane, plane)
        expand = jnp.where(source == iota((256, n), 1), 1.0, 0.0).astype(bf16)
        spread = dot(expand, asked)
        place = iota((256, 128), 0) % cap
        lane = iota((256, 128), 1)
        weight = jnp.where(lane == place, float(SPLIT), jnp.where(lane == place + cap, 1.0, 0.0))
        wanted = jnp.sum(spread * weight, axis=1, keepdims=True).astype(jnp.int32)
        pick[g] = jnp.where(wanted == iota((256, table_rows), 1), 1.0, 0.0).astype(bf16)
        found = dot(pick[g], table[:, :width]).astype(bf16)
        for k in range(group):
            target_send[base + k] = found[k * cap : (k + 1) * cap, :]
        send(target_send, target_recv, base, base + group, 2, False)
    for g in range(n // group):
        base = g * group
        found = dot(pick[g], table[:, width:]).astype(bf16)
        for k in range(group):
            feature_send[base + k] = found[k * cap : (k + 1) * cap, :]
        send(feature_send, feature_recv, base, base + group, 4, False)
    target_recv[me] = target_send[3 * plane]
    feature_recv[me] = feature_send[3 * plane]

    for load in loads[2:]:
        load.wait()
    head = width // HEADS
    queries = HEADS * per_user
    scale = math.log2(math.e) / math.sqrt(head)
    hide = click.shape[1]
    same = iota((width, width), 0) == iota((width, width), 1)
    eye = jnp.where(same, 1.0, 0.0).astype(bf16)

    def turned(x):
        return dot(eye, x, ((1,), (1,))).astype(bf16)

    hidden_t[:hide, :] = turned(click[...])
    hidden_t[hide:, :] = turned(convert[...])
    value_t = turned(value[...])
    for u in range(users):
        first_row = hist[u, :1, :].astype(f32)
        for c in range(seq // CHUNK):
            rows = slice(c * CHUNK, (c + 1) * CHUNK)
            own = hist[u, rows, :]
            made = dot(value_t, own, ((1,), (1,)))
            live = iota((1, CHUNK), 1) < len_ref[u] - c * CHUNK
            keyed[u, :width, rows] = jnp.where(live, made, 0.0).astype(bf16)
            keyed[u, width:, rows] = jnp.where(
                iota((16, CHUNK), 1) < len_ref[u] - c * CHUNK, 1.0, 0.0
            ).astype(bf16)
            live_row = iota((CHUNK, 1), 0) < len_ref[u] - c * CHUNK
            hist[u, rows, :] = jnp.where(live_row, own.astype(f32), first_row).astype(bf16)

    drain(target_recv, 3)
    target = dot(choose, target_recv[...].reshape(n * cap, width)).astype(bf16)
    lane_head = iota((per_user, width), 1) // head

    def query_of(u):
        own = target[u * per_user : (u + 1) * per_user, :]
        return jnp.concatenate(
            [jnp.where(lane_head == h, own, jnp.zeros_like(own)) for h in range(HEADS)], axis=0
        )

    def score(u, c, query, top):
        rows = slice(c * CHUNK, (c + 1) * CHUNK)
        s = dot(hist[u, rows, :], query, ((1,), (1,)))
        scores[u % 2, rows, :] = s
        part = jnp.max(s.reshape(CHUNK // 8, 8, queries), axis=0)
        return part if top is None else jnp.maximum(top, part)

    def weigh(u, c, top):
        rows = slice(c * CHUNK, (c + 1) * CHUNK)
        w = jnp.exp2((scores[u % 2, rows, :] - top) * scale).astype(bf16)
        weights[u % 2, rows, :] = w

    pooled = []

    def interest(u):
        context = dot(keyed[u], weights[u % 2])
        inverse = 1.0 / context[width : width + 1, :]
        parts = []
        for h in range(HEADS):
            tile = slice(h // 2 * 2 * head, (h // 2 + 1) * 2 * head)
            part = context[h * head : (h + 1) * head, tile] * inverse[:, tile]
            parts.append(part if h % 2 == u % 2 else pltpu.roll(part, head, 1))
        raw = jnp.concatenate(parts, axis=0)
        normed = raw * lax.rsqrt(jnp.mean(raw * raw, axis=0, keepdims=True) + 1e-6)
        if u % 2 == 0:
            pooled.append(normed)
        else:
            left = iota((width, 2 * head), 1) < head
            both = jnp.where(left, pooled.pop(), normed)
            interest_t[:, (u - 1) * per_user : (u + 1) * per_user] = both.astype(bf16)

    query = query_of(0)
    top = None
    for c in range(seq // CHUNK):
        top = score(0, c, query, top)
    partial[...] = dot(hidden_t[:, width : 2 * width], target, ((1,), (1,)))
    for u in range(users):
        now = jnp.max(top, axis=0, keepdims=True)
        top = None
        if u + 1 < users:
            query = query_of(u + 1)
        for c in range(seq // CHUNK):
            if u + 1 < users:
                top = score(u + 1, c, query, top)
            weigh(u, c, now)
        interest(u)
    partial[...] += dot(hidden_t[:, :width], interest_t[...])

    drain(feature_recv, 5)
    feature = dot(choose, feature_recv[...].reshape(n * cap, width)).astype(bf16)
    act = partial[...] + dot(hidden_t[:, 2 * width :], feature, ((1,), (1,)))
    act = jnp.maximum(act, 0.0).astype(bf16)
    for i, output_ref in enumerate([click_out_ref, convert_out_ref]):
        logit = dot(output_ref[...].reshape(1, -1), act[i * hide : (i + 1) * hide, :])
        for u in range(users):
            logit_ref[i, u : u + 1, :] = logit[:, u * per_user : (u + 1) * per_user]
    drain(id_send, 0)
    drain(target_send, 2)
    drain(feature_send, 4)


def local(
    n,
    ny,
    history,
    lengths,
    candidates,
    item_table,
    value_weight,
    click_hidden,
    convert_hidden,
    click_output,
    convert_output,
):
    users, per_user = candidates.shape
    seq, width = history.shape[1:]
    total = users * per_user
    cap = max(2 * total // n, 16)
    queries = HEADS * per_user
    slab = pltpu.VMEM((n, cap, width), bf16)
    held = [click_output, convert_output, item_table, history, value_weight, click_hidden, convert_hidden]
    logits = pl.pallas_call(
        functools.partial(fused_kernel, n, ny, cap),
        out_shape=pltpu.VMEM((2, users, per_user), f32),
        in_specs=[pl.BlockSpec(memory_space=pl.ANY)] * 9,
        out_specs=pl.BlockSpec(memory_space=pltpu.VMEM),
        scratch_shapes=[pltpu.VMEM(candidates.shape, jnp.int32), pltpu.SMEM(lengths.shape, jnp.int32)]
        + [pltpu.VMEM(x.shape, x.dtype) for x in held]
        + [
            pltpu.VMEM((n, 1, 128), f32),
            pltpu.VMEM((n, 1, 128), f32),
            pltpu.VMEM((n * cap // 256, 256, item_table.shape[0]), bf16),
            slab,
            slab,
            slab,
            slab,
            pltpu.VMEM((2, seq, queries), f32),
            pltpu.VMEM((2, seq, queries), bf16),
            pltpu.VMEM((users, width + 16, seq), bf16),
            pltpu.VMEM((2 * click_hidden.shape[1], 3 * width), bf16),
            pltpu.VMEM((2 * click_hidden.shape[1], total), f32),
            pltpu.VMEM((width, total), bf16),
            pltpu.SemaphoreType.DMA((8 + users,)),
            pltpu.SemaphoreType.DMA((6,)),
        ],
        compiler_params=pltpu.CompilerParams(collective_id=0, has_side_effects=True),
        name="esmm",
    )(candidates, lengths, *held)
    rate = 1.0 / (1.0 + jnp.exp(-logits[0]))
    return rate, rate / (1.0 + jnp.exp(-logits[1]))


def solution(mesh):
    both = ("gx", "gy")
    placed = (P(both, None, None), P(both), P(both, None), P(both, None), P(), P(), P(), P(), P())
    return jax.shard_map(
        functools.partial(local, mesh.shape["gx"] * mesh.shape["gy"], mesh.shape["gy"]),
        mesh=mesh,
        in_specs=placed,
        out_specs=(P(both, None), P(both, None)),
        check_vma=False,
    )
```

time: 32.5 us -> 28.1 us (0.86)
  the two profiles are of different devices: /device:TPU:13 before, /device:TPU:0 now
where the time goes in v1:
time: 28.1 us; the launch traced here: 27.7 us
  Pallas kernels  26.5 us (94%)
  between operations  0.64 us (2%)
  other arithmetic  0.6 us (2%)
    pallas_call x1, Pallas kernels, local(): pl.pallas_call(functools.partial(fused_kernel, n, ny, cap), out_shape=plt...  26.5 us
    div x1, other arithmetic, local(): return (rate, rate / (1.0 + jnp.exp(-logits[1])))  0.6 us

profile of v1, /device:TPU:0, one launch (start us, length us, event | category | flops | bytes accessed | tf_op | source)
XLA Modules:
  0.0 27.7 jit_solution(3155266016380090641)
XLA Ops:
  0.6 26.5 %esmm.1 = f32[2,4,64]{2,1,0:T(4,128)S(1)} custom-call(s32[4,64]{1,0:T(4,128)} %cand_hbm.1, s32[4]{0:T(128)} %len_hbm.1, bf16[256]{0:T(256)(128)(2,1)} %click_out_hbm.1, bf16[256]{0:T(256)(128)(2,1)} %convert_out_hbm.1, bf16[4096,512]{1,0:T(8,128)(2,1)} %table_hbm.1, bf16[4,2048,256]{2,1,0:T(8,128)(2,1)} %hist_hbm.1, bf16[256,256]{1,0:T(8,128)(2,1)} %value_hbm.1, ...), custom_call_target="tpu_custom_call" | custom-call | tf_op jit(solution)/shard_map/esmm/pallas_call | solution.py:313
  27.1 0.6 %divide_bitcast_fusion = (f32[4,64]{1,0:T(4,128)}, f32[4,64]{1,0:T(4,128)}) fusion(f32[2,4,64]{2,1,0:T(4,128)S(1)} %esmm.1), kind=kLoop, calls=%fused_computation | loop fusion | flops 1792 | bytes 4096 | tf_op jit(solution)/shard_map/div | solution.py:341

commit v2 on v1

--- a/solution.py
+++ b/solution.py
@@ -11,6 +11,7 @@
 HEADS = 4
 CHUNK = 512
 SPLIT = 256
+SHARE = 128
 MESH = pl.DeviceIdType.MESH
 neg_big = -1e30
 f32, bf16 = jnp.float32, jnp.bfloat16
@@ -62,6 +63,8 @@
     interest_t,
     load_sems,
     sems,
+    id_sems,
+    late_sem,
 ):
     me = lax.axis_index("gx") * ny + lax.axis_index("gy")
     users, per_user = cand_ref.shape
@@ -74,20 +77,18 @@
     half = lax.div(me_z, 2)
     planes = (3 - 3 * half, 2 - half, 2 * half + 1 - lax.rem(me_z, 2), me_z)
 
-    def at(q, k):
-        d = planes[q] * plane + lax.rem(me_r + k, plane)
-        return d, (lax.div(d, ny), lax.rem(d, ny))
-
-    def each(lo, hi, body):
-        for q in range(4):
-            first, last = max(lo - q * plane, q // 3), min(hi - q * plane, plane)
-            if first < last:
-                lax.fori_loop(first, last, functools.partial(body, q), 0)
+    def at(q, k, turn=True):
+        r = lax.rem(me_r + k, plane) if turn else k
+        d = planes[q] * plane + r
+        return d, q * plane + r, (lax.div(d, ny), lax.rem(d, ny))
+
+    def each(q, body):
+        lax.fori_loop(q // 3, plane, functools.partial(body, q), 0)
 
     barrier = pltpu.get_barrier_semaphore()
 
-    def greet(q, k, c):
-        pl.semaphore_signal(barrier, inc=1, device_id=at(q, k)[1], device_id_type=MESH)
+    def greet(sem, q, k, c):
+        pl.semaphore_signal(sem, inc=1, device_id=at(q, k)[2], device_id_type=MESH)
         return c
 
     loads = [
@@ -107,9 +108,23 @@
         )
     ]
     loads[0].start()
-    each(0, n, greet)
+    last = me_z == 3
+
+    @pl.when(jnp.logical_not(last))
+    def _():
+        for q in range(3):
+            each(q, functools.partial(greet, barrier))
+
+    each(3, functools.partial(greet, barrier))
     for load in loads[1:]:
         load.start()
+
+    @pl.when(last)
+    def _():
+        pl.semaphore_wait(barrier, n - 1)
+        for q in range(3):
+            each(q, functools.partial(greet, late_sem))
+
     loads[0].wait()
 
     ids = jnp.concatenate([cand_ref[u : u + 1, :] for u in range(users)], axis=1)
@@ -123,73 +138,93 @@
     slot = owner * cap + rank
     high = jnp.where(mine, local // SPLIT, 0).astype(f32).astype(bf16)
     low = jnp.where(mine, local % SPLIT, 0).astype(f32).astype(bf16)
-    rank_i = rank.astype(jnp.int32)
-    lane = iota((128, total), 0)
-    at_high = jnp.where(lane == rank_i, 1.0, 0.0).astype(bf16)
-    at_low = jnp.where(lane == rank_i + cap, 1.0, 0.0).astype(bf16)
-    request = dot(high, at_high, ((1,), (1,))) + dot(low, at_low, ((1,), (1,)))
+    at_rank = jnp.where(iota((128, total), 0) == rank.astype(jnp.int32), 1.0, 0.0).astype(bf16)
+    request = SPLIT * dot(high, at_rank, ((1,), (1,))) + dot(low, at_rank, ((1,), (1,)))
     for d in range(n):
         id_send[d] = request[d : d + 1, :]
 
-    def send(src, dst, lo, hi, sem, by_owner):
-        def one(q, k, c):
-            d, where = at(q, k)
-            pltpu.make_async_remote_copy(
-                src_ref=src.at[d if by_owner else q * plane + k],
-                dst_ref=dst.at[me],
-                send_sem=sems.at[sem],
-                recv_sem=sems.at[sem + 1],
-                device_id=where,
-                device_id_type=MESH,
-            ).start()
-            return c
-
-        each(lo, hi, one)
-
-    others = pl.ds(0, n - 1)
-
-    def drain(ref, sem):
-        pltpu.make_async_copy(ref.at[others], ref.at[others], sems.at[sem]).wait()
-
-    pl.semaphore_wait(barrier, n - 1)
-    send(id_send, id_recv, 0, n, 0, True)
+    def copy_to(where, src, dst, send_sem, recv_sem):
+        pltpu.make_async_remote_copy(
+            src_ref=src,
+            dst_ref=dst,
+            send_sem=send_sem,
+            recv_sem=recv_sem,
+            device_id=where,
+            device_id_type=MESH,
+        ).start()
+
+    def send_ids(q, k, c):
+        d, _, where = at(q, k)
+        copy_to(where, id_send.at[d], id_recv.at[me], sems.at[0], id_sems.at[me_z])
+        return c
+
+    def send_rows(src, dst, sem, turn, q, k, c):
+        _, place, where = at(q, k, turn)
+        copy_to(where, src.at[place], dst.at[me], sems.at[sem], sems.at[sem + 1])
+        return c
+
+    def drain(ref, sem, count=n - 1):
+        some = ref.at[pl.ds(0, count)]
+        pltpu.make_async_copy(some, some, sem).wait()
+
+    @pl.when(last)
+    def _():
+        for q in range(3):
+            each(q, send_ids)
+
+    @pl.when(jnp.logical_not(last))
+    def _():
+        pl.semaphore_wait(barrier, n - 1 - plane)
+
+        @pl.when(half == 0)
+        def _():
+            each(1, send_ids)
+            each(2, send_ids)
+            pl.semaphore_wait(late_sem, plane)
+            each(0, send_ids)
+
+        @pl.when(half == 1)
+        def _():
+            each(0, send_ids)
+            each(1, send_ids)
+            pl.semaphore_wait(late_sem, plane)
+            each(2, send_ids)
+
+    each(3, send_ids)
     id_recv[me] = id_send[me]
 
     same = iota((total, total), 0) == iota((total, total), 1)
     slot_col = jnp.sum(jnp.where(same, slot, 0.0), axis=1, keepdims=True).astype(jnp.int32)
     choose = jnp.where(slot_col == iota((total, n * cap), 1), 1.0, 0.0).astype(bf16)
 
-    drain(id_recv, 1)
-    group = 256 // cap
-    asked = jnp.concatenate([id_recv[d] for d in range(n)], axis=0).astype(bf16)
+    def gather(qs, part, dst):
+        steps = [(q, i) for q in qs for i in range(plane * cap // SHARE)]
+        many = 256 // SHARE
+        for j in range(0, len(steps), many):
+            some = steps[j : j + many]
+            picks, places = [], []
+            for q, i in some:
+                base = q * plane + i * (SHARE // cap)
+                at_rows = slice(base * cap, base * cap + SHARE)
+                if part == 0:
+                    asked = id_recv[pl.ds(planes[q] * plane + i * (SHARE // cap), SHARE // cap)]
+                    spread = jnp.broadcast_to(asked, (SHARE // cap, cap, 128)).reshape(SHARE, 128)
+                    place = iota((SHARE, 128), 0) % cap == iota((SHARE, 128), 1)
+                    wanted = jnp.sum(jnp.where(place, spread, 0.0), axis=1, keepdims=True).astype(jnp.int32)
+                    pick[at_rows, :] = jnp.where(wanted == iota((SHARE, table_rows), 1), 1.0, 0.0).astype(bf16)
+                picks.append(pick[at_rows, :])
+                places += [base + k for k in range(SHARE // cap)]
+            found = dot(jnp.concatenate(picks, axis=0), table[:, part * width : (part + 1) * width]).astype(bf16)
+            for k, at_slot in enumerate(places):
+                dst[at_slot] = found[k * cap : (k + 1) * cap, :]
+
     loads[1].wait()
-    for g in range(n // group):
-        base = g * group
-        turn = base + iota((256, n), 0) // cap
-        quarter = turn // plane
-        source = jnp.where(quarter == 0, planes[0], planes[3])
-        source = jnp.where(quarter == 1, planes[1], jnp.where(quarter == 2, planes[2], source))
-        source = source * plane + lax.rem(me_r + turn % plane, plane)
-        expand = jnp.where(source == iota((256, n), 1), 1.0, 0.0).astype(bf16)
-        spread = dot(expand, asked)
-        place = iota((256, 128), 0) % cap
-        lane = iota((256, 128), 1)
-        weight = jnp.where(lane == place, float(SPLIT), jnp.where(lane == place + cap, 1.0, 0.0))
-        wanted = jnp.sum(spread * weight, axis=1, keepdims=True).astype(jnp.int32)
-        pick[g] = jnp.where(wanted == iota((256, table_rows), 1), 1.0, 0.0).astype(bf16)
-        found = dot(pick[g], table[:, :width]).astype(bf16)
-        for k in range(group):
-            target_send[base + k] = found[k * cap : (k + 1) * cap, :]
-        send(target_send, target_recv, base, base + group, 2, False)
-    for g in range(n // group):
-        base = g * group
-        found = dot(pick[g], table[:, width:]).astype(bf16)
-        for k in range(group):
-            feature_send[base + k] = found[k * cap : (k + 1) * cap, :]
-        send(feature_send, feature_recv, base, base + group, 4, False)
-    target_recv[me] = target_send[3 * plane]
-    feature_recv[me] = feature_send[3 * plane]
-
+    for qs in ((1,), (0,), (2, 3)):
+        for q in qs:
+            drain(id_recv, id_sems.at[planes[q]], plane - q // 3)
+        gather(qs, 0, target_send)
+        for q in qs:
+            each(q, functools.partial(send_rows, target_send, target_recv, 2, q > 0))
     for load in loads[2:]:
         load.wait()
     head = width // HEADS
@@ -205,7 +240,7 @@
     hidden_t[:hide, :] = turned(click[...])
     hidden_t[hide:, :] = turned(convert[...])
     value_t = turned(value[...])
-    for u in range(users):
+    def prepare(u):
         first_row = hist[u, :1, :].astype(f32)
         for c in range(seq // CHUNK):
             rows = slice(c * CHUNK, (c + 1) * CHUNK)
@@ -219,7 +254,18 @@
             live_row = iota((CHUNK, 1), 0) < len_ref[u] - c * CHUNK
             hist[u, rows, :] = jnp.where(live_row, own.astype(f32), first_row).astype(bf16)
 
-    drain(target_recv, 3)
+    for u in range(2):
+        prepare(u)
+    for qs in ((0, 1), (2, 3)):
+        gather(qs, 1, feature_send)
+        for q in qs:
+            each(q, functools.partial(send_rows, feature_send, feature_recv, 4, q > 0))
+    for u in range(2, users):
+        prepare(u)
+    target_recv[me] = target_send[3 * plane + me_r]
+    feature_recv[me] = feature_send[3 * plane + me_r]
+
+    drain(target_recv, sems.at[3])
     target = dot(choose, target_recv[...].reshape(n * cap, width)).astype(bf16)
     lane_head = iota((per_user, width), 1) // head
 
@@ -277,7 +323,7 @@
         interest(u)
     partial[...] += dot(hidden_t[:, :width], interest_t[...])
 
-    drain(feature_recv, 5)
+    drain(feature_recv, sems.at[5])
     feature = dot(choose, feature_recv[...].reshape(n * cap, width)).astype(bf16)
     act = partial[...] + dot(hidden_t[:, 2 * width :], feature, ((1,), (1,)))
     act = jnp.maximum(act, 0.0).astype(bf16)
@@ -285,9 +331,9 @@
         logit = dot(output_ref[...].reshape(1, -1), act[i * hide : (i + 1) * hide, :])
         for u in range(users):
             logit_ref[i, u : u + 1, :] = logit[:, u * per_user : (u + 1) * per_user]
-    drain(id_send, 0)
-    drain(target_send, 2)
-    drain(feature_send, 4)
+    drain(id_send, sems.at[0])
+    drain(target_send, sems.at[2])
+    drain(feature_send, sems.at[4])
 
 
 def local(
@@ -320,7 +366,7 @@
         + [
             pltpu.VMEM((n, 1, 128), f32),
             pltpu.VMEM((n, 1, 128), f32),
-            pltpu.VMEM((n * cap // 256, 256, item_table.shape[0]), bf16),
+            pltpu.VMEM((n * cap, item_table.shape[0]), bf16),
             slab,
             slab,
             slab,
@@ -333,6 +379,8 @@
             pltpu.VMEM((width, total), bf16),
             pltpu.SemaphoreType.DMA((8 + users,)),
             pltpu.SemaphoreType.DMA((6,)),
+            pltpu.SemaphoreType.DMA((4,)),
+            pltpu.SemaphoreType.REGULAR,
         ],
         compiler_params=pltpu.CompilerParams(collective_id=0, has_side_effects=True),
         name="esmm",

time: 28.1 us -> 24.7 us (0.88)
  Pallas kernels: 26.5 us -> 23.3 us
    pallas_call x1, Pallas kernels: 26.5 us -> 23.3 us  [local(): pl.pallas_call(functools.partial(fused_kernel, n, ny, cap), out_shape=plt...]
where the time goes in v2:
time: 24.7 us; the launch traced here: 24.5 us
  Pallas kernels  23.3 us (94%)
  between operations  0.64 us (3%)
  other arithmetic  0.6 us (2%)
    pallas_call x1, Pallas kernels, local(): pl.pallas_call(functools.partial(fused_kernel, n, ny, cap), out_shape=plt...  23.3 us
    div x1, other arithmetic, local(): return (rate, rate / (1.0 + jnp.exp(-logits[1])))  0.6 us

profile of v2, /device:TPU:0, one launch (start us, length us, event | category | flops | bytes accessed | tf_op | source)
XLA Modules:
  0.0 24.5 jit_solution(17740994014321903363)
XLA Ops:
  0.6 23.3 %esmm.1 = f32[2,4,64]{2,1,0:T(4,128)S(1)} custom-call(s32[4,64]{1,0:T(4,128)} %cand_hbm.1, s32[4]{0:T(128)} %len_hbm.1, bf16[256]{0:T(256)(128)(2,1)} %click_out_hbm.1, bf16[256]{0:T(256)(128)(2,1)} %convert_out_hbm.1, bf16[4096,512]{1,0:T(8,128)(2,1)} %table_hbm.1, bf16[4,2048,256]{2,1,0:T(8,128)(2,1)} %hist_hbm.1, bf16[256,256]{1,0:T(8,128)(2,1)} %value_hbm.1, ...), custom_call_target="tpu_custom_call" | custom-call | tf_op jit(solution)/shard_map/esmm/pallas_call | solution.py:359
  23.9 0.6 %divide_bitcast_fusion = (f32[4,64]{1,0:T(4,128)}, f32[4,64]{1,0:T(4,128)}) fusion(f32[2,4,64]{2,1,0:T(4,128)S(1)} %esmm.1), kind=kLoop, calls=%fused_computation | loop fusion | flops 1792 | bytes 4096 | tf_op jit(solution)/shard_map/div | solution.py:389

commit v3 on v2

--- a/solution.py
+++ b/solution.py
@@ -12,6 +12,7 @@
 CHUNK = 512
 SPLIT = 256
 SHARE = 128
+TILE = 512
 MESH = pl.DeviceIdType.MESH
 neg_big = -1e30
 f32, bf16 = jnp.float32, jnp.bfloat16
@@ -83,7 +84,15 @@
         return d, q * plane + r, (lax.div(d, ny), lax.rem(d, ny))
 
     def each(q, body):
-        lax.fori_loop(q // 3, plane, functools.partial(body, q), 0)
+        def eight(c, done):
+            for k in range(8):
+                body(q, c * 8 + k, 0)
+            return done
+
+        for k in range(q // 3, 8):
+            body(q, k, 0)
+        if plane > 8:
+            lax.fori_loop(1, plane // 8, eight, 0)
 
     barrier = pltpu.get_barrier_semaphore()
 
@@ -202,19 +211,31 @@
         many = 256 // SHARE
         for j in range(0, len(steps), many):
             some = steps[j : j + many]
-            picks, places = [], []
+            wanted, at_rows, places = [], [], []
             for q, i in some:
                 base = q * plane + i * (SHARE // cap)
-                at_rows = slice(base * cap, base * cap + SHARE)
+                at_rows.append(slice(base * cap, base * cap + SHARE))
+                places += [base + k for k in range(SHARE // cap)]
                 if part == 0:
                     asked = id_recv[pl.ds(planes[q] * plane + i * (SHARE // cap), SHARE // cap)]
                     spread = jnp.broadcast_to(asked, (SHARE // cap, cap, 128)).reshape(SHARE, 128)
                     place = iota((SHARE, 128), 0) % cap == iota((SHARE, 128), 1)
-                    wanted = jnp.sum(jnp.where(place, spread, 0.0), axis=1, keepdims=True).astype(jnp.int32)
-                    pick[at_rows, :] = jnp.where(wanted == iota((SHARE, table_rows), 1), 1.0, 0.0).astype(bf16)
-                picks.append(pick[at_rows, :])
-                places += [base + k for k in range(SHARE // cap)]
-            found = dot(jnp.concatenate(picks, axis=0), table[:, part * width : (part + 1) * width]).astype(bf16)
+                    wanted.append(jnp.sum(jnp.where(place, spread, 0.0), axis=1, keepdims=True).astype(jnp.int32))
+            found = None
+            for t in range(table_rows // TILE):
+                columns = slice(t * TILE, (t + 1) * TILE)
+                picks = []
+                for i, own in enumerate(at_rows):
+                    if part == 0:
+                        hit = wanted[i] - t * TILE == iota((SHARE, TILE), 1)
+                        picks.append(jnp.where(hit, 1.0, 0.0).astype(bf16))
+                        pick[own, columns] = picks[-1]
+                    else:
+                        picks.append(pick[own, columns])
+                some_rows = table[columns, part * width : (part + 1) * width]
+                more = dot(jnp.concatenate(picks, axis=0), some_rows)
+                found = more if found is None else found + more
+            found = found.astype(bf16)
             for k, at_slot in enumerate(places):
                 dst[at_slot] = found[k * cap : (k + 1) * cap, :]
 
@@ -323,12 +344,18 @@
         interest(u)
     partial[...] += dot(hidden_t[:, :width], interest_t[...])
 
+    ones = jnp.ones((total, total), bf16)
+    out_rows = jnp.concatenate(
+        [dot(jnp.where(same, ref[...].reshape(1, -1), 0.0).astype(bf16), ones) for ref in (click_out_ref, convert_out_ref)],
+        axis=0,
+    )
     drain(feature_recv, sems.at[5])
     feature = dot(choose, feature_recv[...].reshape(n * cap, width)).astype(bf16)
     act = partial[...] + dot(hidden_t[:, 2 * width :], feature, ((1,), (1,)))
     act = jnp.maximum(act, 0.0).astype(bf16)
-    for i, output_ref in enumerate([click_out_ref, convert_out_ref]):
-        logit = dot(output_ref[...].reshape(1, -1), act[i * hide : (i + 1) * hide, :])
+    weighed = act.astype(f32) * out_rows
+    for i in range(2):
+        logit = jnp.sum(weighed[i * hide : (i + 1) * hide, :], axis=0, keepdims=True)
         for u in range(users):
             logit_ref[i, u : u + 1, :] = logit[:, u * per_user : (u + 1) * per_user]
     drain(id_send, sems.at[0])

time: 24.7 us -> 24.3 us (0.984)
  Pallas kernels: 23.3 us -> 22.9 us
    pallas_call x1, Pallas kernels: 23.3 us -> 22.9 us  [local(): pl.pallas_call(functools.partial(fused_kernel, n, ny, cap), out_shape=plt...]
where the time goes in v3:
time: 24.3 us; the launch traced here: 24.1 us
  Pallas kernels  22.9 us (94%)
  between operations  0.64 us (3%)
  other arithmetic  0.6 us (2%)
    pallas_call x1, Pallas kernels, local(): pl.pallas_call(functools.partial(fused_kernel, n, ny, cap), out_shape=plt...  22.9 us
    div x1, other arithmetic, local(): return (rate, rate / (1.0 + jnp.exp(-logits[1])))  0.6 us

profile of v3, /device:TPU:0, one launch (start us, length us, event | category | flops | bytes accessed | tf_op | source)
XLA Modules:
  0.0 24.1 jit_solution(11423056408749162366)
XLA Ops:
  0.6 22.9 %esmm.1 = f32[2,4,64]{2,1,0:T(4,128)S(1)} custom-call(s32[4,64]{1,0:T(4,128)} %cand_hbm.1, s32[4]{0:T(128)} %len_hbm.1, bf16[256]{0:T(256)(128)(2,1)} %click_out_hbm.1, bf16[256]{0:T(256)(128)(2,1)} %convert_out_hbm.1, bf16[4096,512]{1,0:T(8,128)(2,1)} %table_hbm.1, bf16[4,2048,256]{2,1,0:T(8,128)(2,1)} %hist_hbm.1, bf16[256,256]{1,0:T(8,128)(2,1)} %value_hbm.1, ...), custom_call_target="tpu_custom_call" | custom-call | tf_op jit(solution)/shard_map/esmm/pallas_call | solution.py:386
  23.5 0.6 %divide_bitcast_fusion = (f32[4,64]{1,0:T(4,128)}, f32[4,64]{1,0:T(4,128)}) fusion(f32[2,4,64]{2,1,0:T(4,128)S(1)} %esmm.1), kind=kLoop, calls=%fused_computation | loop fusion | flops 1792 | bytes 4096 | tf_op jit(solution)/shard_map/div | solution.py:416
